TPU v7x, 32 devices: a whole 2x2x4 slice. The times are simulated.
32 devices in a mesh: date: 4 (over y, x), pix: 8 (over z, core).
Axes of the slice: x: 2, y: 2, z: 4, core: 2. Of those that a mesh axis runs over, the one named last changes fastest.
Arguments:
- stack: bfloat16 [64, 7, 64, 1024], P('date', None, None, 'pix'), may hold values from -8 to 8
- quality: int32 [64, 64, 1024], P('date', None, 'pix'), may hold values from 0 to 1073741823
- days: int32 [64], P('date'), may hold values from 8 to 1536, as said below
Outputs:
- coef: float32 [7, 8, 64, 1024], P(None, None, 'pix', 'date')
- score: float32 [7, 64, 1024], P(None, 'pix', 'date')
Inputs may be any that keep to these rules, and one draw needn't show every extreme that they name: `days`: strictly increasing.
All inputs are finite; a program needn't handle non-finite values.
Results may differ from a plain program's by a relative error of at most 0.0003.
Values may be sent and summed in bfloat16 or wider, within the bound.
A program may use at most 256 MiB of HBM per device.

v0:
```python
import jax
import jax.numpy as jnp
from jax import lax
from jax.sharding import PartitionSpec as P

RIDGE_TERM = 1.0
PAIR_LIST = [(first, second) for first in range(8) for second in range(first, 8)]


def pair_number(first, second):
    return PAIR_LIST.index((min(first, second), max(first, second)))


def design_matrix(days):
    moment_t = days.astype(jnp.float32)
    columns = [jnp.ones_like(moment_t), (moment_t - 512.0) / 512.0]
    for order in range(1, 4):
        phase = 2.0 * jnp.pi * order * moment_t / 365.25
        columns.append(jnp.cos(phase))
        columns.append(jnp.sin(phase))
    return jnp.stack(columns, 1)


def weights(quality):
    cloud = jnp.bitwise_and(jnp.right_shift(quality, 3), 1)
    level = jnp.bitwise_and(jnp.right_shift(quality, 8), 3)
    return (1 - cloud).astype(jnp.float32) / (1.0 + level.astype(jnp.float32))


def pair_products(design):
    return jnp.stack([design[:, first] * design[:, second] for first, second in PAIR_LIST], 1)


def chol_solve(gram, moment):
    lower = {}
    for first in range(8):
        for second in range(first + 1):
            total = gram[pair_number(first, second)]
            if first == second:
                total = total + RIDGE_TERM
            for inner in range(second):
                total = total - lower[first, inner] * lower[second, inner]
            if first == second:
                lower[first, first] = jnp.sqrt(total)
            else:
                lower[first, second] = total / lower[second, second]
    forward = []
    for first in range(8):
        total = moment[first]
        for inner in range(first):
            total = total - lower[first, inner][None, :] * forward[inner]
        forward.append(total / lower[first, first][None, :])
    backward = [None] * 8
    for first in range(7, -1, -1):
        total = forward[first]
        for inner in range(first + 1, 8):
            total = total - lower[inner, first][None, :] * backward[inner]
        backward[first] = total / lower[first, first][None, :]
    return jnp.stack(backward, 0)


def local(stack, quality, days):
    high = lax.Precision.HIGHEST
    bands = stack.shape[1]
    local_dates, all_rows, arrive_cols = (stack.shape[0], stack.shape[2], stack.shape[3])
    arrive_pixels = all_rows * arrive_cols
    design = design_matrix(days)
    weight = weights(quality).reshape(local_dates, arrive_pixels)
    samples = stack.reshape(local_dates, bands, arrive_pixels).astype(jnp.float32)
    gram_part = jnp.dot(pair_products(design).T, weight, precision=high)
    weighted = weight[:, None, :] * samples
    moment_part = jnp.dot(
        design.T, weighted.reshape(local_dates, bands * arrive_pixels), precision=high
    )
    square_part = jnp.sum(weighted * samples, 0)
    weight_part = jnp.sum(weight, 0)[None, :]
    stacked = jnp.concatenate(
        [gram_part, moment_part.reshape(8 * bands, arrive_pixels), square_part, weight_part], 0
    )
    stacked = stacked.reshape(stacked.shape[0], all_rows, arrive_cols)
    spread = lax.all_to_all(stacked, "pix", split_axis=1, concat_axis=2, tiled=True)
    summed = lax.psum_scatter(spread, "date", scatter_dimension=2, tiled=True)
    row_count, col_count = (summed.shape[1], summed.shape[2])
    pixels = row_count * col_count
    summed = summed.reshape(summed.shape[0], pixels)
    gram = summed[:36]
    moment = summed[36 : 36 + 8 * bands].reshape(8, bands, pixels)
    squares = summed[36 + 8 * bands : 36 + 9 * bands]
    wsum = summed[36 + 9 * bands]
    coef_flat = chol_solve(gram, moment)
    ssr = squares - 2.0 * jnp.sum(coef_flat * moment, 0)
    for first in range(8):
        for second in range(8):
            ssr = (
                ssr
                + gram[pair_number(first, second)][None, :] * coef_flat[first] * coef_flat[second]
            )
    total_ssr, total_weight = lax.psum((jnp.sum(ssr, 1), jnp.sum(wsum)), ("date", "pix"))
    sigma2 = total_ssr / total_weight
    score = jnp.sqrt(ssr / (wsum[None, :] + 1.0)) / jnp.sqrt(sigma2)[:, None]
    coef = jnp.transpose(coef_flat.reshape(8, bands, row_count, col_count), (1, 0, 2, 3))
    return (coef, score.reshape(bands, row_count, col_count))


def solution(mesh):
    return jax.shard_map(
        local,
        mesh=mesh,
        in_specs=(P("date", None, None, "pix"), P("date", None, "pix"), P("date")),
        out_specs=(P(None, None, "pix", "date"), P(None, "pix", "date")),
        check_vma=False,
    )
```

profile of v0, /device:TPU:0, one launch (start us, length us, event | category | flops | bytes accessed | tf_op | source)
XLA Modules:
  0.0 227.7 jit_solution(3004523274341131072)
XLA Ops:
  7.2 1.2 fusion.103
  8.5 2.0 fusion
  11.3 0.3 copy.246
  11.6 0.4 mul.6375
  12.0 3.9 %copy.189 = f32[2,8,7,8192]{3,1,2,0:T(8,128)} copy(f32[2,8,7,8192]{3,2,1,0:T(8,128)S(1)} %bitcast.504) | data formatting | bytes 7340032
  15.9 2.2 convert.1
  18.2 8.7 %fusion.1 = f32[8,57344]{1,0:T(8,128)} fusion(f32[16,8]{1,0:T(8,128)S(1)} %stack.167, f32[16,57344]{1,0:T(8,128)} %bitcast.505, f32[2,8,448,128]{3,2,1,0:T(8,128)} %convert.1), kind=kOutput, calls=%fused_computation.3 | convolution fusion | flops 88997888 | bytes 9175552 | tf_op jit(solution)/shard_map/dot_general | solution.py:72
  26.9 1.8 concatenate.9
  28.7 2.3 %copy.183 = f32[56,64,128]{2,0,1:T(8,128)} copy(f32[56,64,128]{2,1,0:T(8,128)S(1)} %concatenate.9) | data formatting | bytes 3670016 | tf_op jit(solution)/shard_map/concatenate | solution.py:77
  33.5 1.2 fusion.3
  34.8 0.3 pad_maximum_fusion
  35.1 83.3 %all_to_all.18 = f32[100,64,128]{2,0,1:T(8,128)S(1)} all-to-all(f32[100,64,128]{2,0,1:T(8,128)S(1)} %pad_maximum_fusion), channel_id=1, replica_groups=mesh['date'=4,'pix'=8] {'pix'}, dimensions={1} | all-to-all | bytes 6553600 | tf_op jit(solution)/shard_map/all_to_all | solution.py:81
  118.4 2.3 copy.245
  120.7 44.1 %reduce-scatter.2.cloned.1.call-done = f32[100,8,256]{2,1,0:T(8,128)} async-done(((f32[100,8,1024]{2,1,0:T(8,128)}), f32[100,8,256]{2,1,0:T(8,128)}) %reduce-scatter.2.cloned.1.call-update) | async-done | bytes 819216 | tf_op jit(solution)/shard_map/reduce_scatter | solution.py:82
  164.8 0.9 add_bitcast_fusion
  165.7 1.5 slice_reduce_fusion
  167.6 0.9 fusion.104
  168.6 0.8 rsqrt_multiply_fusion.39
  169.4 0.9 rsqrt_multiply_fusion.28
  170.3 0.9 rsqrt_multiply_fusion.26
  171.1 0.9 rsqrt_multiply_fusion.27
  172.0 0.7 rsqrt_multiply_fusion.40
  172.7 0.8 rsqrt_multiply_fusion.18
  173.5 0.8 subtract_sqrt_fusion.7
  174.3 0.8 rsqrt_multiply_fusion.10
  175.1 0.8 subtract_sqrt_fusion.6
  176.7 0.4 divide_dynamic-update-slice_fusion
  178.0 0.9 fusion.93
  179.2 0.8 copy.186
  180.0 39.5 %all-reduce = (f32[7]{0:T(128)S(1)}, f32[]{:T(128)}) all-reduce(f32[7]{0:T(128)S(1)} %get-tuple-element.12, f32[]{:T(128)} %get-tuple-element.192), channel_id=1, replica_groups=mesh['date'=4,'pix'=8] {'date','pix'}, use_global_device_ids=true, to_apply=%region_5.0 | all-reduce | flops 8 | bytes 64 | tf_op jit(solution)/shard_map/psum | solution.py:98
  219.5 0.7 divide_sqrt_fusion
  220.2 0.7 sqrt_divide_fusion
  (130 shorter events, 5.3 us)
Async XLA Ops:
  7.2 3.5 %copy-start.3 = (s32[16]{0:T(128)S(1)}, s32[16]{0:T(128)}, u32[]{:S(2)}) copy-start(s32[16]{0:T(128)} %param.5) | copy-start | bytes 196
  7.2 157.6 %reduce-scatter.2.cloned.1.call-start = ((), (), s32[]{:S(2)}) async-start(), calls=%async_computation.2 | async-start | bytes 4096000 | tf_op jit(solution)/shard_map/reduce_scatter | solution.py:82
  12.0 3.9 %copy-start.1 = (bf16[16,7,64,128]{3,2,1,0:T(8,128)(2,1)S(1)}, bf16[16,7,64,128]{3,2,1,0:T(8,128)(2,1)}, u32[]{:S(2)}) copy-start(bf16[16,7,64,128]{3,2,1,0:T(8,128)(2,1)} %param.3) | copy-start | bytes 5505028
  31.0 3.7 %copy-start.2 = (f32[56,64,128]{2,0,1:T(8,128)S(1)}, f32[56,64,128]{2,0,1:T(8,128)}, u32[]{:S(2)}) copy-start(f32[56,64,128]{2,0,1:T(8,128)} %copy.183) | copy-start | bytes 5505028
  164.8 11.1 %copy-start = (f32[100,8,256]{2,1,0:T(8,128)S(1)}, f32[100,8,256]{2,1,0:T(8,128)}, u32[]{:S(2)}) copy-start(f32[100,8,256]{2,1,0:T(8,128)} %reduce-scatter.2.cloned.1.call-done) | copy-start | bytes 2457604
  176.3 1.4 slice-start
Sparse Core Ops, SparseCore 0:
  120.8 43.9 reduce-scatter.1
where the time goes:
time: 229 us; the launch traced here: 228 us
  blocking collectives  123 us (54%)
  waiting for transfers between devices  44.1 us (19%)
  other arithmetic  19.6 us (9%)
  local copies, waits for them, and re-layouts  16.5 us (7%)
  between operations  14.7 us (6%)
  matrix products  9.93 us (4%)
    all_to_all x1, blocking collectives, local(): lax.all_to_all(stacked, 'pix', split_axis=1, concat_axis=2, tiled=True)  83.3 us
    reduce_scatter x1, waiting for transfers between devices, local(): summed = lax.psum_scatter(spread, 'date', scatter_dimension=2, tiled=True)  44.1 us
    psum x1, blocking collectives, local(): lax.psum((jnp.sum(ssr, 1), jnp.sum(wsum)), ('date', 'pix'))  39.5 us
    dot_general x1, matrix products, local(): jnp.dot(design.T, weighted.reshape(local_dates, bands * arrive_pixels), p...  8.69 us
    div x14, other arithmetic, chol_solve(): lower[first, second] = total / lower[second, second]  5.87 us
    unnamed x54, local copies, waits for them, and re-layouts  5.3 us
  transfers between devices with their start and end apart: 1, of which 1 were waited for; matrix products, arithmetic and copies ran while one was open for 0% of the time, Pallas kernels for 0%

commit v1 on v0

--- a/solution.py
+++ b/solution.py
@@ -95,7 +95,7 @@
                 ssr
                 + gram[pair_number(first, second)][None, :] * coef_flat[first] * coef_flat[second]
             )
-    total_ssr, total_weight = lax.psum((jnp.sum(ssr, 1), jnp.sum(wsum)), ("date", "pix"))
+    total_ssr, total_weight = lax.psum(lax.psum((jnp.sum(ssr, 1), jnp.sum(wsum)), "pix"), "date")
     sigma2 = total_ssr / total_weight
     score = jnp.sqrt(ssr / (wsum[None, :] + 1.0)) / jnp.sqrt(sigma2)[:, None]
     coef = jnp.transpose(coef_flat.reshape(8, bands, row_count, col_count), (1, 0, 2, 3))

time: 229 us -> 216 us (0.943)
  blocking collectives: 123 us -> 110 us
    psum x1 -> x2, blocking collectives: 39.5 us -> 26.3 us  [the longest x1 16.8 us: local(): lax.psum((jnp.sum(ssr, 1), jnp.sum(wsum)), 'pix')]
where the time goes in v1:
time: 216 us; the launch traced here: 215 us
  blocking collectives  110 us (51%)
  waiting for transfers between devices  44.1 us (20%)
  other arithmetic  19.6 us (9%)
  local copies, waits for them, and re-layouts  16.5 us (8%)
  between operations  14.7 us (7%)
  matrix products  9.93 us (5%)
    all_to_all x1, blocking collectives, local(): lax.all_to_all(stacked, 'pix', split_axis=1, concat_axis=2, tiled=True)  83.3 us
    reduce_scatter x1, waiting for transfers between devices, local(): summed = lax.psum_scatter(spread, 'date', scatter_dimension=2, tiled=True)  44.1 us
    psum x1, blocking collectives, local(): lax.psum((jnp.sum(ssr, 1), jnp.sum(wsum)), 'pix')  16.8 us
    psum x1, blocking collectives, local(): lax.psum(lax.psum((jnp.sum(ssr, 1), jnp.sum(wsum)), 'pix'), 'date')  9.54 us
    dot_general x1, matrix products, local(): jnp.dot(design.T, weighted.reshape(local_dates, bands * arrive_pixels), p...  8.69 us
    div x14, other arithmetic, chol_solve(): lower[first, second] = total / lower[second, second]  5.87 us
    unnamed x54, local copies, waits for them, and re-layouts  5.31 us
  transfers between devices with their start and end apart: 1, of which 1 were waited for; matrix products, arithmetic and copies ran while one was open for 0% of the time, Pallas kernels for 0%

profile of v1, /device:TPU:0, one launch (start us, length us, event | category | flops | bytes accessed | tf_op | source)
XLA Modules:
  0.0 214.5 jit_solution(17061088651365330272)
XLA Ops:
  7.2 1.2 fusion.103
  8.5 2.0 fusion
  11.6 0.4 mul.6375
  12.0 3.9 %copy.189 = f32[2,8,7,8192]{3,1,2,0:T(8,128)} copy(f32[2,8,7,8192]{3,2,1,0:T(8,128)S(1)} %bitcast.504) | data formatting | bytes 7340032
  16.0 2.2 %convert.1 = f32[2,8,448,128]{3,2,1,0:T(8,128)} convert(bf16[2,8,448,128]{3,2,1,0:T(8,128)(2,1)S(1)} %bitcast.508) | non-fusion elementwise | flops 917504 | bytes 5505024
  18.3 8.7 %fusion.1 = f32[8,57344]{1,0:T(8,128)} fusion(f32[16,8]{1,0:T(8,128)S(1)} %stack.167, f32[16,57344]{1,0:T(8,128)} %bitcast.505, f32[2,8,448,128]{3,2,1,0:T(8,128)} %convert.1), kind=kOutput, calls=%fused_computation.3 | convolution fusion | flops 88997888 | bytes 9175552 | tf_op jit(solution)/shard_map/dot_general | solution.py:72
  26.9 1.8 concatenate.9
  28.7 2.3 %copy.183 = f32[56,64,128]{2,0,1:T(8,128)} copy(f32[56,64,128]{2,1,0:T(8,128)S(1)} %concatenate.9) | data formatting | bytes 3670016 | tf_op jit(solution)/shard_map/concatenate | solution.py:77
  33.5 1.2 fusion.3
  34.8 0.3 pad_maximum_fusion
  35.1 83.3 %all_to_all.18 = f32[100,64,128]{2,0,1:T(8,128)S(1)} all-to-all(f32[100,64,128]{2,0,1:T(8,128)S(1)} %pad_maximum_fusion), channel_id=1, replica_groups=mesh['date'=4,'pix'=8] {'pix'}, dimensions={1} | all-to-all | bytes 6553600 | tf_op jit(solution)/shard_map/all_to_all | solution.py:81
  118.4 2.3 %copy.245 = f32[100,8,8,128]{3,1,2,0:T(8,128)} copy(f32[100,8,8,128]{3,0,1,2:T(8,128)S(1)} %bitcast.506) | data formatting | bytes 6553600 | tf_op jit(solution)/shard_map/all_to_all | solution.py:81
  120.7 44.1 %reduce-scatter.2.cloned.1.call-done = f32[100,8,256]{2,1,0:T(8,128)} async-done(((f32[100,8,1024]{2,1,0:T(8,128)}), f32[100,8,256]{2,1,0:T(8,128)}) %reduce-scatter.2.cloned.1.call-update) | async-done | bytes 819216 | tf_op jit(solution)/shard_map/reduce_scatter | solution.py:82
  164.8 0.9 add_bitcast_fusion
  165.7 1.5 slice_reduce_fusion
  167.6 0.9 fusion.104
  168.6 0.8 rsqrt_multiply_fusion.39
  169.4 0.9 rsqrt_multiply_fusion.28
  170.3 0.9 rsqrt_multiply_fusion.26
  171.1 0.9 rsqrt_multiply_fusion.27
  172.0 0.7 rsqrt_multiply_fusion.40
  172.7 0.8 rsqrt_multiply_fusion.18
  173.5 0.8 subtract_sqrt_fusion.7
  174.3 0.8 rsqrt_multiply_fusion.10
  175.1 0.8 subtract_sqrt_fusion.6
  176.7 0.4 divide_dynamic-update-slice_fusion
  178.0 0.9 fusion.93
  179.2 0.8 copy.186
  180.0 16.8 %all-reduce = (f32[7]{0:T(128)S(1)}, f32[]{:T(128)}) all-reduce(f32[7]{0:T(128)S(1)} %get-tuple-element.14, f32[]{:T(128)} %get-tuple-element.194), channel_id=1, replica_groups=mesh['date'=4,'pix'=8] {'pix'}, use_global_device_ids=true, to_apply=%region_5.0 | all-reduce | flops 8 | bytes 64 | tf_op jit(solution)/shard_map/psum | solution.py:98
  196.8 9.5 %all-reduce.1 = (f32[7]{0:T(128)S(1)}, f32[]{:T(128)}) all-reduce(f32[7]{0:T(128)S(1)} %get-tuple-element.10, f32[]{:T(128)} %get-tuple-element.11), channel_id=1, replica_groups=mesh['date'=4,'pix'=8] {'date'}, use_global_device_ids=true, to_apply=%region_6.0 | all-reduce | flops 8 | bytes 64 | tf_op jit(solution)/shard_map/psum | solution.py:98
  206.3 0.7 divide_sqrt_fusion
  207.0 0.7 sqrt_divide_fusion
  (131 shorter events, 5.6 us)
Async XLA Ops:
  7.2 3.5 %copy-start.3 = (s32[16]{0:T(128)S(1)}, s32[16]{0:T(128)}, u32[]{:S(2)}) copy-start(s32[16]{0:T(128)} %param.5) | copy-start | bytes 196
  7.2 157.6 %reduce-scatter.2.cloned.1.call-start = ((), (), s32[]{:S(2)}) async-start(), calls=%async_computation.2 | async-start | bytes 4096000 | tf_op jit(solution)/shard_map/reduce_scatter | solution.py:82
  12.0 3.9 %copy-start.1 = (bf16[16,7,64,128]{3,2,1,0:T(8,128)(2,1)S(1)}, bf16[16,7,64,128]{3,2,1,0:T(8,128)(2,1)}, u32[]{:S(2)}) copy-start(bf16[16,7,64,128]{3,2,1,0:T(8,128)(2,1)} %param.3) | copy-start | bytes 5505028
  31.0 3.7 %copy-start.2 = (f32[56,64,128]{2,0,1:T(8,128)S(1)}, f32[56,64,128]{2,0,1:T(8,128)}, u32[]{:S(2)}) copy-start(f32[56,64,128]{2,0,1:T(8,128)} %copy.183) | copy-start | bytes 5505028
  164.8 11.1 %copy-start = (f32[100,8,256]{2,1,0:T(8,128)S(1)}, f32[100,8,256]{2,1,0:T(8,128)}, u32[]{:S(2)}) copy-start(f32[100,8,256]{2,1,0:T(8,128)} %reduce-scatter.2.cloned.1.call-done) | copy-start | bytes 2457604
  176.3 1.4 slice-start
Sparse Core Ops, SparseCore 0:
  120.8 43.9 reduce-scatter.1
